TPU v7x, 32 devices: a whole 2x2x4 slice. The times are simulated.
32 devices in a mesh: ba: 4 (over x, core), ma: 4 (over z), row: 2 (over y).
Axes of the slice: x: 2, y: 2, z: 4, core: 2. Of those that a mesh axis runs over, the one named last changes fastest.
Arguments:
- tokens: bfloat16 [8, 256, 4096], P(('ba', 'row'), None, 'ma'), may hold values from -6 to 6
- attn_gain: bfloat16 [4096], P('ma'), may hold values from 0.25 to 1.75
- query_weight: bfloat16 [4096, 4096], P('row', 'ma'), may hold values from -0.046875 to 0.046875
- key_weight: bfloat16 [4096, 4096], P('row', 'ma'), may hold values from -0.046875 to 0.046875
- value_projection_matrix: bfloat16 [4096, 4096], P('row', 'ma'), may hold values from -0.09375 to 0.09375
- attention_output_matrix: bfloat16 [4096, 4096], P('ma', 'row'), may hold values from -0.125 to 0.125
- bucket_bias_matrix: float32 [32, 64], P(None, 'ma'), may hold values from -6 to 215, as said below
- ffn_gain: bfloat16 [4096], P('ma'), may hold values from 0.25 to 1.75
- gate_weight: bfloat16 [4096, 8192], P(None, ('ma', 'row')), may hold values from -0.09375 to 0.09375
- up_weight: bfloat16 [4096, 8192], P(None, ('ma', 'row')), may hold values from -0.09375 to 0.09375
- down_projection_weight: bfloat16 [8192, 4096], P(('ma', 'row')), may hold values from -0.09375 to 0.09375
Outputs:
- encoded: bfloat16 [8, 256, 4096], P(('ba', 'row'), None, 'ma')
Inputs may be any that keep to these rules, and one draw needn't show every extreme that they name: `bucket_bias_matrix`: entries of the relative position table.
All inputs are finite; a program needn't handle non-finite values.
Results may differ from a plain program's by a relative error of at most 0.017.
Values may be sent and summed in bfloat16 or wider, within the bound.
A program may use at most 128 MiB of HBM per device.

v0:
```python
import jax
import jax.numpy as jnp
from jax import lax
from jax.sharding import PartitionSpec as P

bucket_thresholds = (1, 2, 3, 4, 5, 6, 7, 8, 11, 16, 23, 32, 45, 64, 91, 128)
epsilon = 1e-06


def buckets(length):
    places = jnp.arange(length, dtype=jnp.int32)
    offset = places[None, :] - places[:, None]
    distance = jnp.abs(offset)
    backward = jnp.zeros_like(distance)
    for threshold in bucket_thresholds[:15]:
        backward = backward + (distance >= threshold).astype(jnp.int32)
    forward = jnp.full_like(distance, 15)
    for threshold in bucket_thresholds:
        forward = forward + (distance >= threshold).astype(jnp.int32)
    return jnp.where(offset > 0, forward, backward)


def rms_scale(values, gain):
    mean_square = jnp.mean(values * values, axis=-1, keepdims=True)
    return (values * lax.rsqrt(mean_square + epsilon) * gain.astype(jnp.float32)).astype(
        jnp.bfloat16
    )


def regroup(values, norm_gain_vector):
    widened = (
        lax.all_gather(values, "ma", axis=1, tiled=True),
        lax.all_gather(norm_gain_vector, "ma", axis=1, tiled=True),
    )
    stacked = lax.all_gather(widened[0], "row", axis=0, tiled=True)
    return (stacked, widened[1])


def on_device(
    tokens,
    attn_gain,
    query_weight,
    key_weight,
    value_projection_matrix,
    attention_output_matrix,
    bucket_bias_matrix,
    ffn_gain,
    gate_weight,
    up_weight,
    down_projection_weight,
):
    sequences, length, part_width = tokens.shape
    ma_count = lax.axis_size("ma")
    local_heads = bucket_bias_matrix.shape[1]
    inner_width = query_weight.shape[1]
    head_size = inner_width // local_heads
    slab_rows = sequences * length
    token_rows = tokens.reshape(slab_rows, part_width)
    token_float = token_rows.astype(jnp.float32)
    full_weights = (
        lax.all_gather(query_weight, "row", axis=0, tiled=True),
        lax.all_gather(key_weight, "row", axis=0, tiled=True),
        lax.all_gather(value_projection_matrix, "row", axis=0, tiled=True),
    )
    whole_rows, whole_gain = (
        lax.all_gather(token_rows, "ma", axis=1, tiled=True),
        lax.all_gather(attn_gain.reshape(1, part_width), "ma", axis=1, tiled=True),
    )
    normed = rms_scale(whole_rows.astype(jnp.float32), whole_gain[0])
    projected = tuple(
        (jnp.dot(normed, matrix, preferred_element_type=jnp.float32) for matrix in full_weights)
    )
    query_heads, key_heads, value_heads = [
        member.astype(jnp.bfloat16).reshape(sequences, length, local_heads, head_size)
        for member in projected
    ]
    bucket_grid = buckets(length)
    table_rows = jnp.arange(bucket_bias_matrix.shape[0], dtype=jnp.int32)
    bucket_indicator = (table_rows[:, None, None] == bucket_grid[None, :, :]).astype(jnp.float32)
    relative_position_scores = jnp.einsum(
        "dmy,du->umy", bucket_indicator, bucket_bias_matrix, precision=lax.Precision.HIGHEST
    )
    scores = (
        jnp.einsum("sqhd,skhd->shqk", query_heads, key_heads, preferred_element_type=jnp.float32)
        + relative_position_scores[None]
    )
    row_max = jnp.max(scores, axis=-1, keepdims=True)
    exponent = jnp.exp(scores - row_max)
    weights = (exponent / jnp.sum(exponent, axis=-1, keepdims=True)).astype(jnp.bfloat16)
    attended = jnp.einsum(
        "shqk,skhd->sqhd", weights, value_heads, preferred_element_type=jnp.float32
    )
    attended = attended.astype(jnp.bfloat16).reshape(slab_rows, inner_width)
    partial_out = jnp.dot(
        attended,
        lax.all_gather(attention_output_matrix, "row", axis=1, tiled=True),
        preferred_element_type=jnp.float32,
    )
    attn_out = lax.psum_scatter(
        partial_out.astype(jnp.bfloat16), "ma", scatter_dimension=1, tiled=True
    ).astype(jnp.float32)
    residual_stream = (token_float + attn_out).astype(jnp.bfloat16)
    residual_f = residual_stream.astype(jnp.float32)
    norm_gain_vector = ffn_gain.reshape(1, part_width)
    gate_full, up_full, down_full = (gate_weight, up_weight, down_projection_weight)
    group_rows, group_gain = regroup(residual_stream, norm_gain_vector)
    ffn_in = rms_scale(group_rows.astype(jnp.float32), group_gain[0])
    gate_act = jnp.dot(ffn_in, gate_full, preferred_element_type=jnp.float32)
    up_act = jnp.dot(ffn_in, up_full, preferred_element_type=jnp.float32)
    hidden = (jax.nn.gelu(gate_act, approximate=True) * up_act).astype(jnp.bfloat16)
    down_blocks = down_full.reshape(down_full.shape[0], ma_count, part_width)
    down_terms = jnp.einsum("tf,fmd->mtd", hidden, down_blocks, preferred_element_type=jnp.float32)
    down_terms = down_terms.reshape(ma_count * ffn_in.shape[0], part_width)
    ffn_out = lax.psum_scatter(
        down_terms.astype(jnp.bfloat16), ("ma", "row"), scatter_dimension=0, tiled=True
    ).astype(jnp.float32)
    encoded = (residual_f + ffn_out).astype(jnp.bfloat16)
    return encoded.reshape(sequences, length, part_width)


def solution(mesh):
    in_specs = (
        P(("ba", "row"), None, "ma"),
        P("ma"),
        P("row", "ma"),
        P("row", "ma"),
        P("row", "ma"),
        P("ma", "row"),
        P(None, "ma"),
        P("ma"),
        P(None, ("ma", "row")),
        P(None, ("ma", "row")),
        P(("ma", "row"), None),
    )
    out_specs = P(("ba", "row"), None, "ma")
    return jax.shard_map(
        on_device, mesh=mesh, in_specs=in_specs, out_specs=out_specs, check_vma=False
    )
```

profile of v0, /device:TPU:0, one launch (start us, length us, event | category | flops | bytes accessed | tf_op | source)
XLA Modules:
  0.0 752.7 jit_solution(16300057747724244085)
XLA Ops:
  6.5 0.7 all-gather.23.cloned.1.call-update
  7.3 0.0 all-gather.13.cloned.1.call-start
  7.3 0.7 all-gather.13.cloned.1.call-update
  8.0 0.0 all-gather.15.cloned.1.call-start
  8.1 0.7 all-gather.15.cloned.1.call-update
  8.8 0.0 all-gather.11.cloned.1.call-start
  8.8 0.5 all-gather.11.cloned.1.call-update
  9.3 0.0 all-gather.17.cloned.1.call-start
  9.4 0.5 all-gather.17.cloned.1.call-update
  9.9 0.0 reduce-scatter.3.cloned.1.call-start
  10.0 13.7 %all-gather.1 = bf16[4096]{0:T(1024)(128)(2,1)S(1)} all-gather(bf16[1024]{0:T(1024)(128)(2,1)S(1)} %copy-done.7), channel_id=3, replica_groups=mesh['ba'=4,'ma'=4,'row'=2] {'ma'}, dimensions={0}, use_global_device_ids=true | all-gather | bytes 10240 | tf_op jit(solution)/shard_map/all_gather | solution.py:67
  23.7 0.3 fusion.33
  24.1 4.2 fusion.7
  28.3 5.3 copy.27
  33.6 23.8 %all-gather.23.cloned.1.call-done = bf16[1,256,4096]{2,1,0:T(8,128)(2,1)} async-done(((bf16[1,256,1024]{2,1,0:T(8,128)(2,1)}), bf16[1,256,4096]{2,1,0:T(8,128)(2,1)}) %all-gather.23.cloned.1.call-update) | async-done | bytes 2097168 | tf_op jit(solution)/shard_map/all_gather | solution.py:66
  57.3 2.1 fusion.8
  59.4 102.2 %all-gather.13.cloned.1.call-done = bf16[4096,1024]{1,0:T(8,128)(2,1)} async-done(((bf16[2048,1024]{1,0:T(8,128)(2,1)}), bf16[4096,1024]{1,0:T(8,128)(2,1)}) %all-gather.13.cloned.1.call-update) | async-done | bytes 8388624 | tf_op jit(solution)/shard_map/all_gather | solution.py:61
  161.7 6.4 convolution_convert_fusion.2
  168.1 0.2 copy.25
  168.3 99.0 %all-gather.15.cloned.1.call-done = bf16[4096,1024]{1,0:T(8,128)(2,1)} async-done(((bf16[2048,1024]{1,0:T(8,128)(2,1)}), bf16[4096,1024]{1,0:T(8,128)(2,1)}) %all-gather.15.cloned.1.call-update) | async-done | bytes 8388624 | tf_op jit(solution)/shard_map/all_gather | solution.py:62
  267.3 6.6 convolution_convert_fusion.1
  273.9 1.3 copy.26
  275.2 97.5 %all-gather.11.cloned.1.call-done = bf16[4096,1024]{1,0:T(8,128)(2,1)} async-done(((bf16[2048,1024]{1,0:T(8,128)(2,1)}), bf16[4096,1024]{1,0:T(8,128)(2,1)}) %all-gather.11.cloned.1.call-update) | async-done | bytes 8388624 | tf_op jit(solution)/shard_map/all_gather | solution.py:63
  372.7 6.6 convolution_convert_fusion.3
  379.3 1.3 copy.24
  380.6 3.6 bitcast_add_fusion
  384.3 2.0 copy-done.2
  386.3 0.8 fusion.57
  387.1 5.3 fusion.26
  392.3 85.8 %all-gather.17.cloned.1.call-done = bf16[1024,4096]{1,0:T(8,128)(2,1)} async-done(((bf16[1024,2048]{1,0:T(8,128)(2,1)}), bf16[1024,4096]{1,0:T(8,128)(2,1)}) %all-gather.17.cloned.1.call-update) | async-done | bytes 8388624 | tf_op jit(solution)/shard_map/all_gather | solution.py:96
  478.1 7.2 convolution_convert_fusion
  485.3 0.0 reduce-scatter.3.cloned.1.call-update
  485.4 0.0 all-gather.19.cloned.1.call-start
  485.4 43.7 %reduce-scatter.3.cloned.1.call-done = bf16[256,1024]{1,0:T(8,128)(2,1)} async-done(((bf16[256,4096]{1,0:T(8,128)(2,1)}), bf16[256,1024]{1,0:T(8,128)(2,1)}) %reduce-scatter.3.cloned.1.call-update) | async-done | bytes 524304 | tf_op jit(solution)/shard_map/reduce_scatter | solution.py:99
  529.1 2.0 fusion.30
  531.2 0.0 all-gather.21.cloned.1.call-start
  531.2 45.0 %all-gather.19.cloned.1.call-done = bf16[256,4096]{1,0:T(8,128)(2,1)} async-done(((bf16[256,1024]{1,0:T(8,128)(2,1)}), bf16[256,4096]{1,0:T(8,128)(2,1)}) %all-gather.19.cloned.1.call-update) | async-done | bytes 2097168 | tf_op jit(solution)/shard_map/all_gather | solution.py:32
  576.2 0.0 all-gather.21.cloned.1.call-update
  576.2 0.0 reduce-scatter.5.cloned.1.call-start
  576.3 12.2 %all-gather.2 = bf16[4096]{0:T(1024)(128)(2,1)S(1)} all-gather(bf16[1024]{0:T(1024)(128)(2,1)S(1)} %copy-done.8), channel_id=4, replica_groups=mesh['ba'=4,'ma'=4,'row'=2] {'ma'}, dimensions={0}, use_global_device_ids=true | all-gather | bytes 10240 | tf_op jit(solution)/shard_map/all_gather | solution.py:33
  588.5 44.9 %all-gather.21.cloned.1.call-done = bf16[512,4096]{1,0:T(8,128)(2,1)} async-done(((bf16[256,4096]{1,0:T(8,128)(2,1)}), bf16[512,4096]{1,0:T(8,128)(2,1)}) %all-gather.21.cloned.1.call-update) | async-done | bytes 4194320 | tf_op jit(solution)/shard_map/all_gather | solution.py:35
  633.3 3.2 fusion.1
  636.6 0.2 copy-done.4
  636.8 7.7 %fusion.28 = f32[512,1024]{1,0:T(8,128)S(1)} fusion(bf16[4096,1024]{1,0:T(8,128)(2,1)} %param.19, bf16[512,4096]{1,0:T(8,128)(2,1)S(1)} %copy-done.4, f32[4096]{0:T(1024)S(1)} %mul.97, f32[512]{0:T(512)S(1)} %add_rsqrt_fusion), kind=kOutput, calls=%fused_computation.38 | convolution fusion | flops 4303355904 | bytes 14698496 | tf_op jit(solution)/shard_map/dot_general | solution.py:108
  644.6 4.9 fusion.25
  649.5 6.2 fusion.12
  655.6 88.5 %reduce-scatter.5.cloned.1.call-done = bf16[256,1024]{1,0:T(8,128)(2,1)} async-done(((bf16[2048,1024]{1,0:T(8,128)(2,1)}), bf16[256,1024]{1,0:T(8,128)(2,1)}) %reduce-scatter.5.cloned.1.call-update) | async-done | bytes 524304 | tf_op jit(solution)/shard_map/reduce_scatter | solution.py:114
  744.1 2.0 fusion.31
  (33 shorter events, 0.1 us)
Async XLA Ops:
  6.5 17.5 %copy-start = (f32[32,16]{0,1:T(8,128)S(1)}, f32[32,16]{0,1:T(8,128)}, u32[]{:S(2)}) copy-start(f32[32,16]{0,1:T(8,128)} %param.17) | copy-start | bytes 6148
  6.5 50.8 %all-gather.23.cloned.1.call-start = ((), (), s32[]{:S(2)}) async-start(), calls=%async_computation.10 | async-start | bytes 2621440 | tf_op jit(solution)/shard_map/all_gather | solution.py:66
  7.3 154.4 %all-gather.13.cloned.1.call-start = ((), (), s32[]{:S(2)}) async-start(), calls=%async_computation.3 | async-start | bytes 12582912 | tf_op jit(solution)/shard_map/all_gather | solution.py:61
  8.0 259.3 %all-gather.15.cloned.1.call-start = ((), (), s32[]{:S(2)}) async-start(), calls=%async_computation.4 | async-start | bytes 12582912 | tf_op jit(solution)/shard_map/all_gather | solution.py:62
  8.7 1.2 copy-start.7
  8.8 363.9 %all-gather.11.cloned.1.call-start = ((), (), s32[]{:S(2)}) async-start(), calls=%async_computation.2 | async-start | bytes 12582912 | tf_op jit(solution)/shard_map/all_gather | solution.py:63
  9.3 468.8 %all-gather.17.cloned.1.call-start = ((), (), s32[]{:S(2)}) async-start(), calls=%async_computation.5 | async-start | bytes 12582912 | tf_op jit(solution)/shard_map/all_gather | solution.py:96
  9.9 519.2 %reduce-scatter.3.cloned.1.call-start = ((), (), s32[]{:S(2)}) async-start(), calls=%async_computation.6 | async-start | bytes 2621440 | tf_op jit(solution)/shard_map/reduce_scatter | solution.py:99
  59.4 207.9 %copy-start.6 = (bf16[1,256,4096]{2,1,0:T(8,128)(2,1)S(1)}, bf16[1,256,4096]{2,1,0:T(8,128)(2,1)}, u32[]{:S(2)}) copy-start(bf16[1,256,4096]{2,1,0:T(8,128)(2,1)} %all-gather.23.cloned.1.call-done) | copy-start | bytes 6291460
  384.3 2.1 copy-start.2
  478.1 51.0 %copy-start.5 = (bf16[1,256,1024]{2,1,0:T(8,128)(2,1)S(1)}, bf16[1,256,1024]{2,1,0:T(8,128)(2,1)}, u32[]{:S(2)}) copy-start(bf16[1,256,1024]{2,1,0:T(8,128)(2,1)} %param.11) | copy-start | bytes 1572868
  485.3 91.0 %copy-start.8 = (bf16[1024]{0:T(1024)(128)(2,1)S(1)}, bf16[1024]{0:T(1024)(128)(2,1)}, u32[]{:S(2)}) copy-start(bf16[1024]{0:T(1024)(128)(2,1)} %param.18) | copy-start | bytes 6148
  485.4 90.9 %all-gather.19.cloned.1.call-start = ((), (), s32[]{:S(2)}) async-start(), calls=%async_computation.7 | async-start | bytes 2621440 | tf_op jit(solution)/shard_map/all_gather | solution.py:32
  531.2 102.1 %all-gather.21.cloned.1.call-start = ((), (), s32[]{:S(2)}) async-start(), calls=%async_computation.8 | async-start | bytes 6291456 | tf_op jit(solution)/shard_map/all_gather | solution.py:35
  576.2 167.9 %reduce-scatter.5.cloned.1.call-start = ((), (), s32[]{:S(2)}) async-start(), calls=%async_computation.9 | async-start | bytes 4718592 | tf_op jit(solution)/shard_map/reduce_scatter | solution.py:114
  633.3 3.4 copy-start.4
  633.3 11.2 %slice-start = ((s8[8388608]{0:T(1024)(128)(4,1)}), s8[4194304]{0:T(1024)(128)(4,1)S(1)}, s32[]{:S(2)}) async-start(s8[8388608]{0:T(1024)(128)(4,1)} %bitcast.54), calls=%async_computation.11 | async-start | bytes 8388608
  633.3 16.1 %slice-start.2 = ((s8[8388608]{0:T(1024)(128)(4,1)}), s8[4194304]{0:T(1024)(128)(4,1)S(1)}, s32[]{:S(2)}) async-start(s8[8388608]{0:T(1024)(128)(4,1)} %bitcast.56), calls=%async_computation.13 | async-start | bytes 8388608
  636.8 7.8 %slice-start.1 = ((s8[8388608]{0:T(1024)(128)(4,1)}), s8[4194304]{0:T(1024)(128)(4,1)S(1)}, s32[]{:S(2)}) async-start(s8[8388608]{0:T(1024)(128)(4,1)} %bitcast.54), calls=%async_computation.12 | async-start | bytes 8388608
  636.8 12.7 %slice-start.3 = ((s8[8388608]{0:T(1024)(128)(4,1)}), s8[4194304]{0:T(1024)(128)(4,1)S(1)}, s32[]{:S(2)}) async-start(s8[8388608]{0:T(1024)(128)(4,1)} %bitcast.56), calls=%async_computation.14 | async-start | bytes 8388608
  649.5 96.7 %copy-start.1 = (f32[32,16]{0,1:T(8,128)S(1)}, f32[32,16]{0,1:T(8,128)}, u32[]{:S(2)}) copy-start(f32[32,16]{0,1:T(8,128)} %param.17) | copy-start | bytes 6148
  655.6 88.5 %copy-start.3 = (bf16[256,1024]{1,0:T(8,128)(2,1)S(1)}, bf16[256,1024]{1,0:T(8,128)(2,1)}, u32[]{:S(2)}) copy-start(bf16[256,1024]{1,0:T(8,128)(2,1)} %fusion.30) | copy-start | bytes 1572868
Sparse Core Ops, SparseCore 0:
  8.9 48.3 all-gather.22
  58.9 102.7 all-gather.12
  163.2 104.0 all-gather.14
  268.7 103.9 all-gather.10
  374.1 103.9 all-gather.16
  485.5 43.6 reduce-scatter.2
  531.3 44.8 all-gather.18
  577.8 55.5 all-gather.20
  655.8 88.3 reduce-scatter.4
where the time goes:
time: 753 us
  waiting for transfers between devices  634 us (84%)
  matrix products  58.6 us (8%)
  blocking collectives  25.9 us (3%)
  between operations  13.4 us (2%)
  other arithmetic  10.5 us (1%)
  local copies, waits for them, and re-layouts  10.4 us (1%)
    all_gather x1, waiting for transfers between devices, on_device(): lax.all_gather(query_weight, 'row', axis=0, tiled=True)  102 us
    all_gather x1, waiting for transfers between devices, on_device(): lax.all_gather(key_weight, 'row', axis=0, tiled=True)  99 us
    all_gather x1, waiting for transfers between devices, on_device(): lax.all_gather(value_projection_matrix, 'row', axis=0, tiled=True)  97.5 us
    reduce_scatter x1, waiting for transfers between devices, on_device(): lax.psum_scatter(down_terms.astype(jnp.bfloat16), ('ma', 'row'), scatter_...  88.5 us
    all_gather x1, waiting for transfers between devices, on_device(): lax.all_gather(attention_output_matrix, 'row', axis=1, tiled=True)  85.8 us
    all_gather x1, waiting for transfers between devices, regroup(): lax.all_gather(values, 'ma', axis=1, tiled=True)  45 us
    all_gather x1, waiting for transfers between devices, regroup(): stacked = lax.all_gather(widened[0], 'row', axis=0, tiled=True)  44.9 us
    reduce_scatter x1, waiting for transfers between devices, on_device(): lax.psum_scatter(partial_out.astype(jnp.bfloat16), 'ma', scatter_dimensio...  43.7 us
  transfers between devices with their start and end apart: 9, of which 9 were waited for; matrix products, arithmetic and copies ran while one was open for 6% of the time, Pallas kernels for 0%

commit v1 on v0

--- a/solution.py
+++ b/solution.py
@@ -5,6 +5,19 @@
 
 bucket_thresholds = (1, 2, 3, 4, 5, 6, 7, 8, 11, 16, 23, 32, 45, 64, 91, 128)
 epsilon = 1e-06
+
+
+def ring_gather(x, axis, dim):
+    size, mine, span = (lax.axis_size(axis), lax.axis_index(axis), x.shape[dim])
+    right = [(i, (i + 1) % size) for i in range(size)]
+    out = jnp.zeros((*x.shape[:dim], size * span, *x.shape[dim + 1 :]), x.dtype)
+    carried = x
+    for step in range(size):
+        source = (mine - step) % size
+        out = lax.dynamic_update_slice_in_dim(out, carried, source * span, axis=dim)
+        if step < size - 1:
+            carried = lax.ppermute(carried, axis, right)
+    return out
 
 
 def buckets(length):
@@ -29,7 +42,7 @@
 
 def regroup(values, norm_gain_vector):
     widened = (
-        lax.all_gather(values, "ma", axis=1, tiled=True),
+        ring_gather(values, "ma", 1),
         lax.all_gather(norm_gain_vector, "ma", axis=1, tiled=True),
     )
     stacked = lax.all_gather(widened[0], "row", axis=0, tiled=True)

time: 753 us -> 752 us (level)
    all_gather x1 -> x0, waiting for transfers between devices: 45 us -> none  [regroup(): lax.all_gather(values, 'ma', axis=1, tiled=True)]
    ppermute x0 -> x3, waiting for transfers between devices: none -> 41.2 us  [ring_gather(): carried = lax.ppermute(carried, axis, right)]
  transfers between devices with their start and end apart: 9 -> 11, of which waited for: 9 -> 11; matrix products, arithmetic and copies ran while one was open for 6% -> 6% of each run, Pallas kernels for 0% -> 0%
where the time goes in v1:
time: 752 us; the launch traced here: 751 us
  waiting for transfers between devices  628 us (84%)
  matrix products  58.6 us (8%)
  blocking collectives  25.9 us (3%)
  local copies, waits for them, and re-layouts  14.3 us (2%)
  between operations  13.7 us (2%)
  other arithmetic  9.75 us (1%)
    all_gather x1, waiting for transfers between devices, on_device(): lax.all_gather(query_weight, 'row', axis=0, tiled=True)  102 us
    all_gather x1, waiting for transfers between devices, on_device(): lax.all_gather(key_weight, 'row', axis=0, tiled=True)  99 us
    all_gather x1, waiting for transfers between devices, on_device(): lax.all_gather(value_projection_matrix, 'row', axis=0, tiled=True)  97.5 us
    reduce_scatter x1, waiting for transfers between devices, on_device(): lax.psum_scatter(down_terms.astype(jnp.bfloat16), ('ma', 'row'), scatter_...  88.5 us
    all_gather x1, waiting for transfers between devices, on_device(): lax.all_gather(attention_output_matrix, 'row', axis=1, tiled=True)  85.8 us
    reduce_scatter x1, waiting for transfers between devices, on_device(): lax.psum_scatter(partial_out.astype(jnp.bfloat16), 'ma', scatter_dimensio...  43.7 us
    all_gather x1, waiting for transfers between devices, regroup(): stacked = lax.all_gather(widened[0], 'row', axis=0, tiled=True)  42.8 us
    ppermute x3, waiting for transfers between devices, ring_gather(): carried = lax.ppermute(carried, axis, right)  41.2 us
  transfers between devices with their start and end apart: 11, of which 11 were waited for; matrix products, arithmetic and copies ran while one was open for 6% of the time, Pallas kernels for 0%

profile of v1, /device:TPU:0, one launch (start us, length us, event | category | flops | bytes accessed | tf_op | source)
XLA Modules:
  0.0 750.9 jit_solution(8895643880934201229)
XLA Ops:
  6.5 0.7 all-gather.20.cloned.1.call-update
  7.3 0.7 all-gather.12.cloned.1.call-update
  8.1 0.7 all-gather.14.cloned.1.call-update
  8.8 0.5 all-gather.10.cloned.1.call-update
  9.4 0.5 all-gather.16.cloned.1.call-update
  9.9 0.0 reduce-scatter.3.cloned.1.call-start
  10.0 13.7 %all-gather.1 = bf16[4096]{0:T(1024)(128)(2,1)S(1)} all-gather(bf16[1024]{0:T(1024)(128)(2,1)S(1)} %copy-done.7), channel_id=3, replica_groups=mesh['ba'=4,'ma'=4,'row'=2] {'ma'}, dimensions={0}, use_global_device_ids=true | all-gather | bytes 10240 | tf_op jit(solution)/shard_map/all_gather | solution.py:80
  23.7 0.3 fusion.33
  24.1 4.2 fusion.7
  28.3 5.3 copy.27
  33.6 23.7 %all-gather.20.cloned.1.call-done = bf16[1,256,4096]{2,1,0:T(8,128)(2,1)} async-done(((bf16[1,256,1024]{2,1,0:T(8,128)(2,1)}), bf16[1,256,4096]{2,1,0:T(8,128)(2,1)}) %all-gather.20.cloned.1.call-update) | async-done | bytes 2097168 | tf_op jit(solution)/shard_map/all_gather | solution.py:79
  57.3 2.1 fusion.8
  59.4 102.2 %all-gather.12.cloned.1.call-done = bf16[4096,1024]{1,0:T(8,128)(2,1)} async-done(((bf16[2048,1024]{1,0:T(8,128)(2,1)}), bf16[4096,1024]{1,0:T(8,128)(2,1)}) %all-gather.12.cloned.1.call-update) | async-done | bytes 8388624 | tf_op jit(solution)/shard_map/all_gather | solution.py:74
  161.7 6.4 convolution_convert_fusion.2
  168.1 0.2 copy.25
  168.3 99.0 %all-gather.14.cloned.1.call-done = bf16[4096,1024]{1,0:T(8,128)(2,1)} async-done(((bf16[2048,1024]{1,0:T(8,128)(2,1)}), bf16[4096,1024]{1,0:T(8,128)(2,1)}) %all-gather.14.cloned.1.call-update) | async-done | bytes 8388624 | tf_op jit(solution)/shard_map/all_gather | solution.py:75
  267.3 6.6 convolution_convert_fusion.1
  273.9 1.3 copy.26
  275.2 97.5 %all-gather.10.cloned.1.call-done = bf16[4096,1024]{1,0:T(8,128)(2,1)} async-done(((bf16[2048,1024]{1,0:T(8,128)(2,1)}), bf16[4096,1024]{1,0:T(8,128)(2,1)}) %all-gather.10.cloned.1.call-update) | async-done | bytes 8388624 | tf_op jit(solution)/shard_map/all_gather | solution.py:76
  372.7 6.6 convolution_convert_fusion.3
  379.3 1.3 copy.24
  380.6 3.6 bitcast_add_fusion
  384.3 2.0 copy-done.2
  386.3 0.8 fusion.58
  387.1 5.3 fusion.26
  392.3 85.8 %all-gather.16.cloned.1.call-done = bf16[1024,4096]{1,0:T(8,128)(2,1)} async-done(((bf16[1024,2048]{1,0:T(8,128)(2,1)}), bf16[1024,4096]{1,0:T(8,128)(2,1)}) %all-gather.16.cloned.1.call-update) | async-done | bytes 8388624 | tf_op jit(solution)/shard_map/all_gather | solution.py:109
  478.1 7.2 convolution_convert_fusion
  485.3 0.0 all-gather.18.cloned.1.call-start
  485.4 43.7 %reduce-scatter.3.cloned.1.call-done = bf16[256,1024]{1,0:T(8,128)(2,1)} async-done(((bf16[256,4096]{1,0:T(8,128)(2,1)}), bf16[256,1024]{1,0:T(8,128)(2,1)}) %reduce-scatter.3.cloned.1.call-update) | async-done | bytes 524304 | tf_op jit(solution)/shard_map/reduce_scatter | solution.py:112
  529.1 0.2 broadcast_in_dim.5
  529.3 1.3 constant_dynamic-update-slice_fusion.3
  530.6 0.7 collective-permute-start
  531.3 14.4 %collective-permute-done = bf16[256,1024]{1,0:T(8,128)(2,1)S(1)} collective-permute-done((bf16[256,1024]{1,0:T(8,128)(2,1)S(1)}, bf16[256,1024]{1,0:T(8,128)(2,1)S(1)}, u32[]{:S(2)}, u32[]{:S(2)}) %collective-permute-start) | collective-permute-done | bytes 524320 | tf_op jit(solution)/shard_map/ppermute | solution.py:19
  545.7 14.3 %collective-permute-done.1 = bf16[256,1024]{1,0:T(8,128)(2,1)} collective-permute-done((bf16[256,1024]{1,0:T(8,128)(2,1)S(1)}, bf16[256,1024]{1,0:T(8,128)(2,1)}, u32[]{:S(2)}, u32[]{:S(2)}) %collective-permute-start.1) | collective-permute-done | bytes 524320 | tf_op jit(solution)/shard_map/ppermute | solution.py:19
  560.1 1.1 constant_dynamic-update-slice_fusion.1
  561.2 12.5 %collective-permute-done.2 = bf16[256,1024]{1,0:T(8,128)(2,1)} collective-permute-done((bf16[256,1024]{1,0:T(8,128)(2,1)}, bf16[256,1024]{1,0:T(8,128)(2,1)}, u32[]{:S(2)}, u32[]{:S(2)}) %collective-permute-start.2) | collective-permute-done | bytes 524320 | tf_op jit(solution)/shard_map/ppermute | solution.py:19
  573.7 1.1 constant_dynamic-update-slice_fusion
  574.7 1.3 copy-done.3
  576.1 0.0 reduce-scatter.5.cloned.1.call-start
  576.2 12.2 %all-gather.2 = bf16[4096]{0:T(1024)(128)(2,1)S(1)} all-gather(bf16[1024]{0:T(1024)(128)(2,1)S(1)} %copy-done.8), channel_id=4, replica_groups=mesh['ba'=4,'ma'=4,'row'=2] {'ma'}, dimensions={0}, use_global_device_ids=true | all-gather | bytes 10240 | tf_op jit(solution)/shard_map/all_gather | solution.py:46
  588.3 42.8 %all-gather.18.cloned.1.call-done = bf16[512,4096]{1,0:T(8,128)(2,1)} async-done(((bf16[256,4096]{1,0:T(8,128)(2,1)}), bf16[512,4096]{1,0:T(8,128)(2,1)}) %all-gather.18.cloned.1.call-update) | async-done | bytes 4194320 | tf_op jit(solution)/shard_map/all_gather | solution.py:48
  631.1 3.2 fusion.1
  634.4 0.2 copy-done.4
  634.6 7.7 %fusion.28 = f32[512,1024]{1,0:T(8,128)S(1)} fusion(bf16[4096,1024]{1,0:T(8,128)(2,1)} %param.19, bf16[512,4096]{1,0:T(8,128)(2,1)S(1)} %copy-done.4, f32[4096]{0:T(1024)S(1)} %mul.113, f32[512]{0:T(512)S(1)} %add_rsqrt_fusion), kind=kOutput, calls=%fused_computation.38 | convolution fusion | flops 4303355904 | bytes 14698496 | tf_op jit(solution)/shard_map/dot_general | solution.py:121
  642.4 4.9 fusion.25
  647.3 6.2 fusion.12
  653.5 88.5 %reduce-scatter.5.cloned.1.call-done = bf16[256,1024]{1,0:T(8,128)(2,1)} async-done(((bf16[2048,1024]{1,0:T(8,128)(2,1)}), bf16[256,1024]{1,0:T(8,128)(2,1)}) %reduce-scatter.5.cloned.1.call-update) | async-done | bytes 524304 | tf_op jit(solution)/shard_map/reduce_scatter | solution.py:127
  742.0 2.0 fusion.31
  (40 shorter events, 0.3 us)
Async XLA Ops:
  6.5 17.5 %copy-start = (f32[32,16]{0,1:T(8,128)S(1)}, f32[32,16]{0,1:T(8,128)}, u32[]{:S(2)}) copy-start(f32[32,16]{0,1:T(8,128)} %param.17) | copy-start | bytes 6148
  6.5 50.8 %all-gather.20.cloned.1.call-start = ((), (), s32[]{:S(2)}) async-start(), calls=%async_computation.9 | async-start | bytes 2621440 | tf_op jit(solution)/shard_map/all_gather | solution.py:79
  7.3 154.4 %all-gather.12.cloned.1.call-start = ((), (), s32[]{:S(2)}) async-start(), calls=%async_computation.3 | async-start | bytes 12582912 | tf_op jit(solution)/shard_map/all_gather | solution.py:74
  8.0 259.3 %all-gather.14.cloned.1.call-start = ((), (), s32[]{:S(2)}) async-start(), calls=%async_computation.4 | async-start | bytes 12582912 | tf_op jit(solution)/shard_map/all_gather | solution.py:75
  8.7 1.2 copy-start.7
  8.8 363.9 %all-gather.10.cloned.1.call-start = ((), (), s32[]{:S(2)}) async-start(), calls=%async_computation.2 | async-start | bytes 12582912 | tf_op jit(solution)/shard_map/all_gather | solution.py:76
  9.3 468.8 %all-gather.16.cloned.1.call-start = ((), (), s32[]{:S(2)}) async-start(), calls=%async_computation.5 | async-start | bytes 12582912 | tf_op jit(solution)/shard_map/all_gather | solution.py:109
  9.9 519.2 %reduce-scatter.3.cloned.1.call-start = ((), (), s32[]{:S(2)}) async-start(), calls=%async_computation.6 | async-start | bytes 2621440 | tf_op jit(solution)/shard_map/reduce_scatter | solution.py:112
  59.4 207.9 %copy-start.6 = (bf16[1,256,4096]{2,1,0:T(8,128)(2,1)S(1)}, bf16[1,256,4096]{2,1,0:T(8,128)(2,1)}, u32[]{:S(2)}) copy-start(bf16[1,256,4096]{2,1,0:T(8,128)(2,1)} %all-gather.20.cloned.1.call-done) | copy-start | bytes 6291460
  384.3 2.1 copy-start.2
  485.3 44.1 %copy-start.5 = (bf16[1,256,1024]{2,1,0:T(8,128)(2,1)S(1)}, bf16[1,256,1024]{2,1,0:T(8,128)(2,1)}, u32[]{:S(2)}) copy-start(bf16[1,256,1024]{2,1,0:T(8,128)(2,1)} %param.11) | copy-start | bytes 1572868
  485.3 145.8 %all-gather.18.cloned.1.call-start = ((), (), s32[]{:S(2)}) async-start(), calls=%async_computation.7 | async-start | bytes 6291456 | tf_op jit(solution)/shard_map/all_gather | solution.py:48
  529.3 46.8 %copy-start.8 = (bf16[1024]{0:T(1024)(128)(2,1)S(1)}, bf16[1024]{0:T(1024)(128)(2,1)}, u32[]{:S(2)}) copy-start(bf16[1024]{0:T(1024)(128)(2,1)} %param.18) | copy-start | bytes 6148
  530.6 15.1 %collective-permute-start = (bf16[256,1024]{1,0:T(8,128)(2,1)S(1)}, bf16[256,1024]{1,0:T(8,128)(2,1)S(1)}, u32[]{:S(2)}, u32[]{:S(2)}) collective-permute-start(bf16[256,1024]{1,0:T(8,128)(2,1)S(1)} %get-tuple-element.6), channel_id=1, source_target_pairs={{0,2},{2,4},{4,6},{6,0},{1,3},{3,5},{5,7},{7,1},{8,10},{10,12},{12... | collective-permute-start | bytes 1572872 | tf_op jit(solution)/shard_map/ppermute | solution.py:19
  545.7 14.3 %collective-permute-start.1 = (bf16[256,1024]{1,0:T(8,128)(2,1)S(1)}, bf16[256,1024]{1,0:T(8,128)(2,1)}, u32[]{:S(2)}, u32[]{:S(2)}) collective-permute-start(bf16[256,1024]{1,0:T(8,128)(2,1)S(1)} %collective-permute-done), channel_id=1, source_target_pairs={{0,2},{2,4},{4,6},{6,0},{1,3},{3,5},{5,7},{7,1},{8,10},{10,12},{12... | collective-permute-start | bytes 1572872 | tf_op jit(solution)/shard_map/ppermute | solution.py:19
  560.0 13.6 %collective-permute-start.2 = (bf16[256,1024]{1,0:T(8,128)(2,1)}, bf16[256,1024]{1,0:T(8,128)(2,1)}, u32[]{:S(2)}, u32[]{:S(2)}) collective-permute-start(bf16[256,1024]{1,0:T(8,128)(2,1)} %collective-permute-done.1), channel_id=1, source_target_pairs={{0,2},{2,4},{4,6},{6,0},{1,3},{3,5},{5,7},{7,1},{8,10},{10,12},{12... | collective-permute-start | bytes 1572872 | tf_op jit(solution)/shard_map/ppermute | solution.py:19
  574.7 1.3 copy-start.3
  576.1 165.9 %reduce-scatter.5.cloned.1.call-start = ((), (), s32[]{:S(2)}) async-start(), calls=%async_computation.8 | async-start | bytes 4718592 | tf_op jit(solution)/shard_map/reduce_scatter | solution.py:127
  631.1 3.4 copy-start.4
  631.1 11.2 %slice-start = ((s8[8388608]{0:T(1024)(128)(4,1)}), s8[4194304]{0:T(1024)(128)(4,1)S(1)}, s32[]{:S(2)}) async-start(s8[8388608]{0:T(1024)(128)(4,1)} %bitcast.55), calls=%async_computation.10 | async-start | bytes 8388608
  631.1 16.1 %slice-start.2 = ((s8[8388608]{0:T(1024)(128)(4,1)}), s8[4194304]{0:T(1024)(128)(4,1)S(1)}, s32[]{:S(2)}) async-start(s8[8388608]{0:T(1024)(128)(4,1)} %bitcast.57), calls=%async_computation.12 | async-start | bytes 8388608
  634.6 7.8 %slice-start.1 = ((s8[8388608]{0:T(1024)(128)(4,1)}), s8[4194304]{0:T(1024)(128)(4,1)S(1)}, s32[]{:S(2)}) async-start(s8[8388608]{0:T(1024)(128)(4,1)} %bitcast.55), calls=%async_computation.11 | async-start | bytes 8388608
  634.6 12.7 %slice-start.3 = ((s8[8388608]{0:T(1024)(128)(4,1)}), s8[4194304]{0:T(1024)(128)(4,1)S(1)}, s32[]{:S(2)}) async-start(s8[8388608]{0:T(1024)(128)(4,1)} %bitcast.57), calls=%async_computation.13 | async-start | bytes 8388608
  647.3 96.8 %copy-start.1 = (f32[32,16]{0,1:T(8,128)S(1)}, f32[32,16]{0,1:T(8,128)}, u32[]{:S(2)}) copy-start(f32[32,16]{0,1:T(8,128)} %param.17) | copy-start | bytes 6148
Sparse Core Ops, SparseCore 0:
  8.9 48.3 all-gather.19
  58.9 102.7 all-gather.11
  163.2 104.0 all-gather.13
  268.7 103.9 all-gather.9
  374.1 103.9 all-gather.15
  485.4 43.6 reduce-scatter.2
  576.2 54.8 all-gather.17
  653.6 88.3 reduce-scatter.4
